TPU v7x, 32 devices: a whole 2x2x4 slice. The times are simulated.
32 devices in a mesh: env: 4 (over y, core), dof: 8 (over z, x).
Axes of the slice: x: 2, y: 2, z: 4, core: 2. Of those that a mesh axis runs over, the one named last changes fastest.
Arguments:
- system_matrix: bfloat16 [8, 8192, 8192], P('env', 'dof'), parts along dimension 0, as said below
- forces: float32 [8192, 8, 128], P('dof', 'env'), parts along dimension 1, may hold values from -6 to 6
Outputs:
- accelerations: float32 [8192, 8, 128], P('dof', 'env'), parts along dimension 1
- residual: float32 [8192, 8, 128], P('dof', 'env'), parts along dimension 1
There are 4 independent parts, one for each index of `env`. A program takes and returns all parts, laid end to end along the dimension named above; each array names one. Nothing has to cross between parts.
Inputs may be any that keep to these rules, and one draw needn't show every extreme that they name: `system_matrix`: each environment's matrix is exactly symmetric and positive definite.
All inputs are finite; a program needn't handle non-finite values.
Results may differ from a plain program's by a relative error of at most 0.012.
Values may be sent and summed in bfloat16 or wider, within the bound.
A program may use at most 128 MiB of HBM per device.

v0:
```python
import functools

import jax
import jax.numpy as jnp
from jax import lax
from jax.experimental import pallas as pl
from jax.experimental.pallas import tpu as pltpu
from jax.sharding import PartitionSpec as P

ITERS = 4
MESH = pl.DeviceIdType.MESH


def ring_order(n):
    width = 1
    while (2 * width) ** 2 <= n:
        width *= 2
    depth = n // width
    if width == 1 or depth % 2:
        return list(range(n))
    order = [z * width for z in range(depth)]
    for turn, z in enumerate(reversed(range(depth))):
        xs = list(range(1, width))
        order += [z * width + x for x in (xs if turn % 2 == 0 else xs[::-1])]
    return order


def lookup(table, index):
    value = jnp.int32(0)
    for place, entry in enumerate(table):
        value = value + jnp.where(index == place, jnp.int32(entry), jnp.int32(0))
    return value


def kernel(n, envs, rows, a_hbm, f_ref, x_ref, r_ref, a_vmem, field, direction, image, sums,
           load_sem, send_sem, recv_sem, sum_send, sum_recv):
    order = ring_order(n)
    inverse = [order.index(i) for i in range(n)]
    me = lax.axis_index("dof")
    place = lookup(inverse, me)
    half = rows // 2
    far = n // 2
    tile = min(128, rows)

    def owner(step):
        return lookup(order, lax.rem(place + step + n, n))

    following, previous = owner(1), owner(-1)

    def load(env, block):
        return pltpu.make_async_copy(
            a_hbm.at[env, :, pl.ds(pl.multiple_of(block * rows, rows), rows)],
            a_vmem.at[env, block],
            load_sem.at[env, block],
        )

    def hop(env, way, block, part, target):
        return pltpu.make_async_remote_copy(
            src_ref=field.at[env, block, part],
            dst_ref=field.at[env, block, part],
            send_sem=send_sem.at[env, way, block, part],
            recv_sem=recv_sem.at[env, block, part],
            device_id={"dof": target},
            device_id_type=MESH,
        )

    def forward(env, block, part):
        return hop(env, 0, block, part, following)

    def backward(env, block, part):
        return hop(env, 1, block, part, previous)

    def share(env, slot, peer, source):
        return pltpu.make_async_remote_copy(
            src_ref=sums.at[env, slot, source],
            dst_ref=sums.at[env, slot, source],
            send_sem=sum_send.at[env, slot, peer],
            recv_sem=sum_recv.at[env, slot, source],
            device_id={"dof": peer},
            device_id_type=MESH,
        )

    def peer_of(j):
        return lax.rem(me + j, n)

    def add(env, block, part, first=False):
        product = jnp.dot(
            a_vmem[env, block, :, part * half:(part + 1) * half],
            field[env, block, part],
            preferred_element_type=jnp.float32,
        )
        if first:
            image[env] = product
        else:
            image[env] += product

    def start_own(env):
        for q in range(2):
            forward(env, me, q).start()
            backward(env, me, 1 - q).start()

    def begin(env, k):
        @pl.when(k == 0)
        def _():
            load(env, me).wait()
        add(env, me, 0, first=True)
        add(env, me, 1)

    def near(env, k, s, relay):
        before, after = owner(-s), owner(s)
        for q in range(2):
            forward(env, before, q).wait_recv()
            if relay > q:
                forward(env, before, q).start()
            backward(env, after, 1 - q).wait_recv()
            if relay > q:
                backward(env, after, 1 - q).start()
            if q == 0:
                @pl.when(k == 0)
                def _():
                    load(env, before).wait()
                    load(env, after).wait()
            if relay == 1 and q == 0:
                yield
            add(env, before, q)
            add(env, after, 1 - q)

    def gather(env, k, between):
        begin(env, k)

        def step(s, carry):
            for _ in near(env, k, s, 2):
                pass
            return carry

        lax.fori_loop(1, far - 1, step, 0)
        for _ in near(env, k, far - 1, 1):
            between()
        block = owner(far)
        forward(env, block, 0).wait_recv()

        @pl.when(k == 0)
        def _():
            load(env, block).wait()
        add(env, block, 0)
        backward(env, block, 1).wait_recv()
        add(env, block, 1)

        def drain(s, carry):
            for q in range(2):
                forward(env, owner(-s), q).wait_send()
                backward(env, owner(s), q).wait_send()
            return carry

        lax.fori_loop(0, far - 1, drain, 0)
        forward(env, owner(1 - far), 0).wait_send()
        backward(env, owner(far - 1), 1).wait_send()

    def local_sums(env, k):
        slot = lax.rem(k, 2)

        def step(i, carry):
            at = pl.ds(pl.multiple_of(i * tile, tile), tile)
            r, d, q = r_ref[env, at, :], direction[env, at, :], image[env, at, :]
            fold = lambda v: jnp.sum(v.reshape(tile // 8, 8, v.shape[-1]), axis=0)
            return tuple(c + fold(v) for c, v in zip(carry, (r * r, d * q, r * q, q * q)))

        zero = jnp.zeros((8, image.shape[-1]), jnp.float32)
        totals = lax.fori_loop(0, rows // tile, step, (zero,) * 4)
        for i, total in enumerate(totals):
            sums[env, slot, me, i:i + 1, :] = jnp.sum(total, axis=0, keepdims=True)

        def send(j, carry):
            share(env, slot, peer_of(j), me).start()
            return carry

        lax.fori_loop(1, n, send, 0)

    def update(env, k):
        slot = lax.rem(k, 2)

        def receive(j, carry):
            share(env, slot, me, peer_of(j)).wait_recv()
            share(env, slot, peer_of(j), me).wait_send()
            return carry

        lax.fori_loop(1, n, receive, 0)
        total = sums[env, slot, 0]
        for j in range(1, n):
            total = total + sums[env, slot, j]
        now, curve, cross, square = (total[i:i + 1, :] for i in range(4))
        alpha = now / curve
        beta = (now - 2.0 * alpha * cross + alpha * alpha * square) / now

        def step(i, carry):
            at = pl.ds(pl.multiple_of(i * tile, tile), tile)
            d = direction[env, at, :]
            x_ref[env, at, :] = x_ref[env, at, :] + alpha * d
            r = r_ref[env, at, :] - alpha * image[env, at, :]
            r_ref[env, at, :] = r
            d = r + beta * d
            direction[env, at, :] = d
            put(env, i, d)
            return carry

        lax.fori_loop(0, rows // tile, step, 0)

    def put(env, i, d):
        per = half // tile if half >= tile else 1
        narrow = d.astype(field.dtype)
        if half >= tile:
            at = pl.ds(pl.multiple_of(lax.rem(i, per) * tile, tile), tile)
            field[env, me, i // per, at, :] = narrow
        else:
            for q in range(2):
                field[env, me, q] = narrow[q * half:(q + 1) * half]

    barrier = pltpu.get_barrier_semaphore()

    def greet(j, carry):
        pl.semaphore_signal(barrier, inc=1, device_id={"dof": peer_of(j)}, device_id_type=MESH)
        return carry

    def copy_in(env):
        def step(i, carry):
            at = pl.ds(pl.multiple_of(i * tile, tile), tile)
            f = f_ref[env, at, :]
            x_ref[env, at, :] = jnp.zeros_like(f)
            r_ref[env, at, :] = f
            direction[env, at, :] = f
            put(env, i, f)
            return carry
        lax.fori_loop(0, rows // tile, step, 0)

    lax.fori_loop(1, n, greet, 0)
    copy_in(0)
    for env in range(envs):
        load(env, me).start()

        def fetch(s, carry):
            load(env, owner(-s)).start()
            load(env, owner(s)).start()
            return carry

        lax.fori_loop(1, far, fetch, 0)
        load(env, owner(far)).start()
    pl.semaphore_wait(barrier, n - 1)
    start_own(0)
    copy_in(1)

    def iteration(k, carry):
        def second():
            @pl.when(k > 0)
            def _():
                update(1, k - 1)
            start_own(1)

        def first():
            update(0, k)

            @pl.when(k < ITERS - 1)
            def _():
                start_own(0)

        gather(0, k, second)
        local_sums(0, k)
        gather(1, k, first)
        local_sums(1, k)
        return carry

    lax.fori_loop(0, ITERS, iteration, 0)
    update(1, ITERS - 1)


def solution(mesh):
    n = mesh.shape["dof"]

    def on_device(system_matrix, forces):
        envs, rows, _ = system_matrix.shape
        rhs = forces.shape[-1]
        block = jax.ShapeDtypeStruct((envs, rows, rhs), jnp.float32)
        vmem = pl.BlockSpec(memory_space=pltpu.VMEM)
        x, r = pl.pallas_call(
            functools.partial(kernel, n, envs, rows),
            out_shape=(block, block),
            in_specs=[pl.BlockSpec(memory_space=pl.ANY), vmem],
            out_specs=(vmem, vmem),
            scratch_shapes=[
                pltpu.VMEM((envs, n, rows, rows), jnp.bfloat16),
                pltpu.VMEM((envs, n, 2, rows // 2, rhs), jnp.bfloat16),
                pltpu.VMEM((envs, rows, rhs), jnp.float32),
                pltpu.VMEM((envs, rows, rhs), jnp.float32),
                pltpu.VMEM((envs, 2, n, 4, rhs), jnp.float32),
                pltpu.SemaphoreType.DMA((envs, n)),
                pltpu.SemaphoreType.DMA((envs, 2, n, 2)),
                pltpu.SemaphoreType.DMA((envs, n, 2)),
                pltpu.SemaphoreType.DMA((envs, 2, n)),
                pltpu.SemaphoreType.DMA((envs, 2, n)),
            ],
            compiler_params=pltpu.CompilerParams(
                collective_id=0, has_side_effects=True, vmem_limit_bytes=60 * 1024 * 1024
            ),
        )(system_matrix, forces.transpose(1, 0, 2))
        return x.transpose(1, 0, 2), r.transpose(1, 0, 2)

    return jax.shard_map(
        on_device,
        mesh=mesh,
        in_specs=(P("env", "dof", None), P("dof", "env", None)),
        out_specs=(P("dof", "env", None), P("dof", "env", None)),
        check_vma=False,
    )
```

profile of v0, /device:TPU:0, one launch (start us, length us, event | category | flops | bytes accessed | tf_op | source)
XLA Modules:
  0.0 184.7 jit_solution(15022841667054797928)
XLA Ops:
  0.6 2.3 %copy.8 = f32[1024,2,128]{2,0,1:T(8,128)} copy(f32[1024,2,128]{2,1,0:T(2,128)} %param.3) | data formatting | bytes 2097152 | tf_op args[1]
  2.9 175.8 %shard_map.41 = (f32[2,1024,128]{2,1,0:T(8,128)}, f32[2,1024,128]{2,1,0:T(8,128)}) custom-call(bf16[2,1024,8192]{2,1,0:T(8,128)(2,1)} %a_hbm.1, f32[2,1024,128]{2,1,0:T(8,128)} %bitcast.5), custom_call_target="tpu_custom_call" | custom-call | tf_op jit(solution)/shard_map/pallas_call | solution.py:283
  178.7 3.0 %copy.5 = f32[1024,2,128]{2,1,0:T(2,128)} copy(f32[1024,2,128]{2,0,1:T(8,128)} %bitcast.7) | data formatting | bytes 2097152
  181.7 3.0 %copy.6 = f32[1024,2,128]{2,1,0:T(2,128)} copy(f32[1024,2,128]{2,0,1:T(8,128)} %bitcast.6) | data formatting | bytes 2097152
where the time goes:
time: 185 us
  Pallas kernels  176 us (95%)
  local copies, waits for them, and re-layouts  8.27 us (4%)
    pallas_call x1, Pallas kernels, on_device(): pl.pallas_call(functools.partial(kernel, n, envs, rows), out_shape=(block...  176 us
    unnamed x3, local copies, waits for them, and re-layouts  8.27 us

commit v1 on v0

--- a/solution.py
+++ b/solution.py
@@ -31,8 +31,25 @@
         value = value + jnp.where(index == place, jnp.int32(entry), jnp.int32(0))
     return value
 
-
-def kernel(n, envs, rows, a_hbm, f_ref, x_ref, r_ref, a_vmem, field, direction, image, sums,
+PIECES = 4
+LADDER = (2, 4)
+GATHER = (
+    (1, 2, 50, 145, 26, 137, 3, 36, 25, 43, 44, 52, 19, 60, 5, 38, 46, 27, 10, 13, 30, 22, 21, 23, 29, 31, 7, 15),
+    (160, 67, 100, 136, 75, 108, 116, 184, 219, 92, 102, 5, 144, 110, 145, 149, 126, 29, 1, 9, 86, 13, 87, 19, 95, 25, 7, 15),
+)
+SCATTER = (
+    (7, 15, 535, 543, 5, 10, 13, 21, 534, 29, 542, 515, 19, 539, 1, 514, 25, 538, 137, 550, 558, 548, 555, 556, 564, 145, 572, 562),
+    (7, 15, 531, 1, 5, 265, 13, 25, 541, 149, 599, 95, 598, 67, 401, 614, 638, 400, 622, 219, 612, 416, 440, 75, 620, 392, 628, 604),
+)
+OWN_SEND = ((5, 5, 5, 5), (7, 5, 6, 7))
+OWN_TAKE = ((5, 5, 5, 5), (7, 5, 6, 7))
+LEAVES = (18, 8)
+GATHER_TURN = 20
+SCATTER_TURN = 28
+GROUP = 4
+
+
+def ring_kernel(n, envs, rows, a_hbm, f_ref, x_ref, r_ref, a_vmem, field, direction, image, sums,
            load_sem, send_sem, recv_sem, sum_send, sum_recv):
     order = ring_order(n)
     inverse = [order.index(i) for i in range(n)]
@@ -272,36 +289,479 @@
     update(1, ITERS - 1)
 
 
+def ladder_kernel(n, depth, rows, a_hbm, f_ref, x_out, r_out, a_gather, a_scatter,
+                  field, inbox, outbox, narrow, parts, xg, rg, dg, image, xs, rs, ds, drawn, sums,
+                  load_sem, gather_send, gather_recv, scatter_send, scatter_recv, sum_send, sum_recv):
+    width = 2
+    rhs = image.shape[-1]
+    piece = rows // PIECES
+    tile = min(128, rows)
+    me = lax.axis_index("dof")
+    core = lax.rem(lax.axis_index("env"), 2)
+    other = 1 - core
+    x = lax.rem(me, width)
+    z = me // width
+    high = z // (depth // 2)
+    place = z + high * (depth - 1 - 2 * z)
+    inward = 1 - 2 * high
+    targets = (me + 1 - 2 * x, me - width * inward, me + width * inward)
+    near_slot, far_slot = (3 - inward) // 2, (3 + inward) // 2
+    take_slot = (jnp.int32(0), near_slot, far_slot)
+    give_slot = (jnp.int32(0), far_slot, near_slot)
+
+    def by_place(pair):
+        return jnp.where(place == 1, jnp.int32(pair[1]), jnp.int32(pair[0]))
+
+    def node(r):
+        level = r // width
+        return (level + high * (depth - 1 - 2 * level)) * width + lax.rem(x + lax.rem(r, width), width)
+
+    plans = [
+        [by_place([t[i] + 1024 * t[i + 1] for t in tables]) for i in range(0, len(tables[0]), 2)]
+        for tables in (GATHER, SCATTER)
+    ]
+
+    def read_plan(kind, pair):
+        word = jnp.int32(0)
+        for spot, value in enumerate(plans[kind]):
+            word = word + jnp.where(pair == spot, value, jnp.int32(0))
+        return [
+            (node(lax.rem(entry, 8)), lax.rem(entry // 8, 4), lax.rem(entry // 32, 8), entry // 256)
+            for entry in (lax.rem(word, 1024), word // 1024)
+        ]
+
+    def for_bits(mask, body):
+        for d in range(3):
+            @pl.when(lax.rem(mask // (1 << d), 2) == 1)
+            def _(d=d):
+                body(d)
+
+    def load(kind, block, q):
+        env, buffer = ((core, a_gather), (other, a_scatter))[kind]
+        return pltpu.make_async_copy(
+            a_hbm.at[env, :, pl.ds(pl.multiple_of(block * rows + q * piece, piece), piece)],
+            buffer.at[block, q],
+            load_sem.at[kind, block, q],
+        )
+
+    def spread(block, q, d, k):
+        return pltpu.make_async_remote_copy(
+            src_ref=field.at[lax.rem(k, 2), block, q],
+            dst_ref=field.at[lax.rem(k, 2), block, q],
+            send_sem=gather_send.at[block, q, d],
+            recv_sem=gather_recv.at[block, q],
+            device_id={"dof": targets[d]},
+            device_id_type=MESH,
+        )
+
+    def collect(block, q, slot, target):
+        return pltpu.make_async_remote_copy(
+            src_ref=outbox.at[block, q],
+            dst_ref=inbox.at[block, q, slot],
+            send_sem=scatter_send.at[block, q],
+            recv_sem=scatter_recv.at[block, q, slot],
+            device_id={"dof": target},
+            device_id_type=MESH,
+        )
+
+    def share(kind, peer, source):
+        return pltpu.make_async_remote_copy(
+            src_ref=sums.at[kind, source],
+            dst_ref=sums.at[kind, source],
+            send_sem=sum_send.at[kind, peer],
+            recv_sem=sum_recv.at[kind, source],
+            device_id={"dof": peer},
+            device_id_type=MESH,
+        )
+
+    def peer_of(j):
+        return lax.rem(me + j, n)
+
+    def send_field(block, q, mask, k):
+        def one(d):
+            @pl.when(k > 0)
+            def _():
+                spread(block, q, d, k - 1).wait_send()
+            spread(block, q, d, k).start()
+        for_bits(mask, one)
+
+    def gather_start(k):
+        for q in range(PIECES):
+            send_field(me, q, by_place([t[q] for t in OWN_SEND]), k)
+
+    def loaded(kind, blocks, k):
+        @pl.when(k == 0)
+        def _():
+            for block, q in blocks:
+                load(kind, block, q).wait()
+
+    def times(block, q, k):
+        return jnp.dot(a_gather[block, q], field[lax.rem(k, 2), block, q], preferred_element_type=jnp.float32)
+
+    def gather_own(k):
+        loaded(0, [(me, q) for q in range(PIECES)], k)
+        image[...] = functools.reduce(jnp.add, [times(me, q, k) for q in range(PIECES)])
+
+    def gather_steps(lo, hi, k):
+        def group(g, carry):
+            blocks = []
+            for j in range(GROUP // 2):
+                for block, q, mask, _ in read_plan(0, g * (GROUP // 2) + j):
+                    spread(block, q, 0, k).wait_recv()
+                    send_field(block, q, mask, k)
+                    blocks.append((block, q))
+            loaded(0, blocks, k)
+            products = [times(block, q, k) for block, q in blocks]
+            image[...] += functools.reduce(jnp.add, products)
+            return carry
+
+        lax.fori_loop(lo // GROUP, hi // GROUP, group, 0)
+
+    def gather_drain():
+        for q in range(PIECES):
+            for_bits(by_place([t[q] for t in OWN_SEND]), lambda d: spread(me, q, d, ITERS - 1).wait_send())
+
+        def step(i, carry):
+            for block, q, mask, _ in read_plan(0, i):
+                for_bits(mask, lambda d: spread(block, q, d, ITERS - 1).wait_send())
+            return carry
+
+        lax.fori_loop(0, len(GATHER[0]) // 2, step, 0)
+
+    def part(block, q):
+        return jnp.dot(narrow[...], a_scatter[block, q], preferred_element_type=jnp.float32)
+
+    def take(block, q, mask, total):
+        def one(d):
+            collect(block, q, take_slot[d], me).wait_recv()
+            total[...] += inbox[block, q, take_slot[d]].astype(jnp.float32)
+        for_bits(mask, one)
+
+    def give(block, q, parent, value, k):
+        @pl.when(k > 0)
+        def _():
+            collect(block, q, 0, targets[0]).wait_send()
+        outbox[block, q] = value.astype(outbox.dtype)
+        for d in range(3):
+            @pl.when(parent == d)
+            def _(d=d):
+                collect(block, q, give_slot[d], targets[d]).start()
+
+    def scatter_leaves(k):
+        def group(g, carry):
+            entries = read_plan(1, g)
+            loaded(1, [(block, q) for block, q, _, _ in entries], k)
+            values = [part(block, q) for block, q, _, _ in entries]
+            for (block, q, _, parent), value in zip(entries, values):
+                give(block, q, parent, value, k)
+            return carry
+
+        lax.fori_loop(0, leaves // 2, group, 0)
+
+    def scatter_parts(k):
+        def group(g, carry):
+            entries = read_plan(1, g)
+            loaded(1, [(block, q) for block, q, _, _ in entries], k)
+            for j, (block, q, _, _) in enumerate(entries):
+                parts[2 * g + j] = part(block, q)
+            return carry
+
+        lax.fori_loop(leaves // 2, len(SCATTER[0]) // 2, group, 0)
+        loaded(1, [(me, q) for q in range(PIECES)], k)
+        for q in range(PIECES):
+            drawn[q] = part(me, q)
+
+    def scatter_steps(lo, hi, k):
+        def step(i, carry):
+            for j, (block, q, mask, parent) in enumerate(read_plan(1, i)):
+                take(block, q, mask, parts.at[2 * i + j])
+                give(block, q, parent, parts[2 * i + j], k)
+            return carry
+
+        lax.fori_loop(lo // 2, hi // 2, step, 0)
+
+    def scatter_own():
+        for q in range(PIECES):
+            take(me, q, by_place([t[q] for t in OWN_TAKE]), drawn.at[q])
+
+    def scatter_drain():
+        def step(i, carry):
+            for block, q, _, _ in read_plan(1, i):
+                collect(block, q, 0, targets[0]).wait_send()
+            return carry
+
+        lax.fori_loop(0, len(SCATTER[0]) // 2, step, 0)
+
+    def send_sums(kind, rows_of):
+        for i, total in enumerate(rows_of):
+            sums[kind, me, i:i + 1, :] = total
+
+        def send(j, carry):
+            share(kind, peer_of(j), me).start()
+            return carry
+
+        lax.fori_loop(1, n, send, 0)
+
+    def gather_sums():
+        def step(i, carry):
+            at = pl.ds(pl.multiple_of(i * tile, tile), tile)
+            r, d, q = rg[at, :], dg[at, :], image[at, :]
+            fold = lambda v: jnp.sum(v.reshape(tile // 8, 8, rhs), axis=0)
+            return tuple(c + fold(v) for c, v in zip(carry, (r * r, d * q, r * q, q * q)))
+
+        zero = jnp.zeros((8, rhs), jnp.float32)
+        totals = lax.fori_loop(0, rows // tile, step, (zero,) * 4)
+        send_sums(0, [jnp.sum(total, axis=0, keepdims=True) for total in totals])
+
+    def cuts():
+        for q in range(PIECES):
+            for j in range(piece // rhs):
+                yield q, slice(j * rhs, (j + 1) * rhs), q * piece + j * rhs
+
+    def scatter_sums():
+        totals = [jnp.zeros((rhs, rhs), jnp.float32)] * 4
+        for q, lanes, _ in cuts():
+            r, d, v = rs[q, :, lanes], ds[q, :, lanes], drawn[q, :, lanes]
+            totals = [c + w for c, w in zip(totals, (r * r, d * v, r * v, v * v))]
+        send_sums(1, [jnp.sum(total.T, axis=0, keepdims=True) for total in totals])
+
+    def ratios(kind):
+        def receive(j, carry):
+            share(kind, me, peer_of(j)).wait_recv()
+            share(kind, peer_of(j), me).wait_send()
+            return carry
+
+        lax.fori_loop(1, n, receive, 0)
+        total = sums[kind, 0]
+        for j in range(1, n):
+            total = total + sums[kind, j]
+        now, curve, cross, square = (total[i:i + 1, :] for i in range(4))
+        alpha = now / curve
+        beta = (now - 2.0 * alpha * cross + alpha * alpha * square) / now
+        return alpha, beta
+
+    def gather_update(later):
+        alpha, beta = ratios(0)
+        for q in range(PIECES):
+            at = slice(q * piece, (q + 1) * piece)
+            d = dg[at, :]
+            xg[at, :] = xg[at, :] + alpha * d
+            r = rg[at, :] - alpha * image[at, :]
+            rg[at, :] = r
+            d = r + beta * d
+            dg[at, :] = d
+            field[lax.rem(later, 2), me, q] = d.astype(field.dtype)
+
+    def scatter_update():
+        alpha, beta = (jnp.broadcast_to(v, (rhs, rhs)).T for v in ratios(1))
+        for q, lanes, at in cuts():
+            d = ds[q, :, lanes]
+            xs[q, :, lanes] = xs[q, :, lanes] + alpha * d
+            r = rs[q, :, lanes] - alpha * drawn[q, :, lanes]
+            rs[q, :, lanes] = r
+            d = r + beta * d
+            ds[q, :, lanes] = d
+            narrow[:, at:at + rhs] = d.astype(narrow.dtype)
+
+    def strided(env, start, size):
+        return pl.ds(env + 2 * start, size, stride=2)
+
+    barrier = pltpu.get_barrier_semaphore()
+
+    def greet(j, carry):
+        pl.semaphore_signal(barrier, inc=1, device_id={"dof": peer_of(j)}, device_id_type=MESH)
+        return carry
+
+    lax.fori_loop(1, n, greet, 0)
+    leaves = by_place(LEAVES)
+
+    def fetch(kind, i):
+        block = node(i if kind == 0 else n - 1 - i)
+        for q in range(PIECES):
+            load(kind, block, q).start()
+
+    def fetch_all(first):
+        def body(i, carry):
+            fetch(first, i)
+            return carry
+
+        lax.fori_loop(0, n, body, 0)
+
+    @pl.when(core == 0)
+    def _():
+        fetch_all(0)
+        fetch_all(1)
+
+    @pl.when(core == 1)
+    def _():
+        fetch_all(1)
+        fetch_all(0)
+
+    for q in range(PIECES):
+        at = slice(q * piece, (q + 1) * piece)
+        f = f_ref[strided(core, q * piece, piece), :]
+        xg[at, :] = jnp.zeros_like(f)
+        rg[at, :] = f
+        dg[at, :] = f
+        field[0, me, q] = f.astype(field.dtype)
+    for q, lanes, at in cuts():
+        f = f_ref[strided(other, at, rhs), :].T
+        xs[q, :, lanes] = jnp.zeros_like(f)
+        rs[q, :, lanes] = f
+        ds[q, :, lanes] = f
+        narrow[:, at:at + rhs] = f.astype(narrow.dtype)
+
+    pl.semaphore_wait(barrier, n - 1)
+    turns = 2 * ITERS
+
+    @pl.when(core == 0)
+    def _():
+        gather_start(jnp.int32(0))
+        gather_own(jnp.int32(0))
+
+    @pl.when(core == 1)
+    def _():
+        scatter_leaves(jnp.int32(0))
+
+    def phase(t, carry):
+        k, later = t // 2, (t + 1) // 2
+        kind = lax.rem(t + core, 2)
+
+        @pl.when(kind == 0)
+        def _():
+            gather_steps(0, GATHER_TURN, k)
+
+            @pl.when(t > 0)
+            def _():
+                scatter_update()
+
+            @pl.when(t < turns - 1)
+            def _():
+                scatter_leaves(later)
+            gather_steps(GATHER_TURN, len(GATHER[0]), k)
+            gather_sums()
+
+        @pl.when(kind == 1)
+        def _():
+            scatter_parts(k)
+            scatter_steps(leaves, SCATTER_TURN, k)
+
+            @pl.when(t > 0)
+            def _():
+                gather_update(later)
+
+            @pl.when(t < turns - 1)
+            def _():
+                gather_start(later)
+                gather_own(later)
+            scatter_steps(SCATTER_TURN, len(SCATTER[0]), k)
+            scatter_own()
+            scatter_sums()
+        return carry
+
+    lax.fori_loop(0, turns, phase, 0)
+    gather_drain()
+    scatter_drain()
+
+    @pl.when(core == 0)
+    def _():
+        scatter_update()
+
+    @pl.when(core == 1)
+    def _():
+        gather_update(jnp.int32(ITERS))
+    x_out[strided(core, 0, rows), :] = xg[...]
+    r_out[strided(core, 0, rows), :] = rg[...]
+    for q, lanes, at in cuts():
+        x_out[strided(other, at, rhs), :] = xs[q, :, lanes].T
+        r_out[strided(other, at, rhs), :] = rs[q, :, lanes].T
+
+
+def ladder(n, depth, system_matrix, forces):
+    envs, rows, _ = system_matrix.shape
+    rhs = forces.shape[-1]
+    piece = rows // PIECES
+    flat = jax.ShapeDtypeStruct((rows * envs, rhs), jnp.float32)
+    vmem = pl.BlockSpec(memory_space=pltpu.VMEM)
+    tall = pltpu.VMEM((rows, rhs), jnp.float32)
+    wide = pltpu.VMEM((PIECES, rhs, piece), jnp.float32)
+    x, r = pl.pallas_call(
+        functools.partial(ladder_kernel, n, depth, rows),
+        out_shape=(flat, flat),
+        in_specs=[pl.BlockSpec(memory_space=pl.ANY), vmem],
+        out_specs=(vmem, vmem),
+        scratch_shapes=[
+            pltpu.VMEM((n, PIECES, rows, piece), jnp.bfloat16),
+            pltpu.VMEM((n, PIECES, rows, piece), jnp.bfloat16),
+            pltpu.VMEM((2, n, PIECES, piece, rhs), jnp.bfloat16),
+            pltpu.VMEM((n, PIECES, 3, rhs, piece), jnp.bfloat16),
+            pltpu.VMEM((n, PIECES, rhs, piece), jnp.bfloat16),
+            pltpu.VMEM((rhs, rows), jnp.bfloat16),
+            pltpu.VMEM((len(SCATTER[0]), rhs, piece), jnp.float32),
+            tall, tall, tall, tall,
+            wide, wide, wide, wide,
+            pltpu.VMEM((2, n, 4, rhs), jnp.float32),
+            pltpu.SemaphoreType.DMA((2, n, PIECES)),
+            pltpu.SemaphoreType.DMA((n, PIECES, 3)),
+            pltpu.SemaphoreType.DMA((n, PIECES)),
+            pltpu.SemaphoreType.DMA((n, PIECES)),
+            pltpu.SemaphoreType.DMA((n, PIECES, 3)),
+            pltpu.SemaphoreType.DMA((2, n)),
+            pltpu.SemaphoreType.DMA((2, n)),
+        ],
+        compiler_params=pltpu.CompilerParams(
+            collective_id=0, has_side_effects=True, vmem_limit_bytes=62 * 1024 * 1024
+        ),
+    )(system_matrix, forces.reshape(rows * envs, rhs))
+    return x.reshape(rows, envs, rhs), r.reshape(rows, envs, rhs)
+
+
+def ring(n, system_matrix, forces):
+    envs, rows, _ = system_matrix.shape
+    rhs = forces.shape[-1]
+    block = jax.ShapeDtypeStruct((envs, rows, rhs), jnp.float32)
+    vmem = pl.BlockSpec(memory_space=pltpu.VMEM)
+    x, r = pl.pallas_call(
+        functools.partial(ring_kernel, n, envs, rows),
+        out_shape=(block, block),
+        in_specs=[pl.BlockSpec(memory_space=pl.ANY), vmem],
+        out_specs=(vmem, vmem),
+        scratch_shapes=[
+            pltpu.VMEM((envs, n, rows, rows), jnp.bfloat16),
+            pltpu.VMEM((envs, n, 2, rows // 2, rhs), jnp.bfloat16),
+            pltpu.VMEM((envs, rows, rhs), jnp.float32),
+            pltpu.VMEM((envs, rows, rhs), jnp.float32),
+            pltpu.VMEM((envs, 2, n, 4, rhs), jnp.float32),
+            pltpu.SemaphoreType.DMA((envs, n)),
+            pltpu.SemaphoreType.DMA((envs, 2, n, 2)),
+            pltpu.SemaphoreType.DMA((envs, n, 2)),
+            pltpu.SemaphoreType.DMA((envs, 2, n)),
+            pltpu.SemaphoreType.DMA((envs, 2, n)),
+        ],
+        compiler_params=pltpu.CompilerParams(
+            collective_id=0, has_side_effects=True, vmem_limit_bytes=60 * 1024 * 1024
+        ),
+    )(system_matrix, forces.transpose(1, 0, 2))
+    return x.transpose(1, 0, 2), r.transpose(1, 0, 2)
+
+
+def grid_of(n):
+    width = 1
+    while (2 * width) ** 2 <= n:
+        width *= 2
+    return width, n // width
+
+
 def solution(mesh):
     n = mesh.shape["dof"]
 
     def on_device(system_matrix, forces):
         envs, rows, _ = system_matrix.shape
         rhs = forces.shape[-1]
-        block = jax.ShapeDtypeStruct((envs, rows, rhs), jnp.float32)
-        vmem = pl.BlockSpec(memory_space=pltpu.VMEM)
-        x, r = pl.pallas_call(
-            functools.partial(kernel, n, envs, rows),
-            out_shape=(block, block),
-            in_specs=[pl.BlockSpec(memory_space=pl.ANY), vmem],
-            out_specs=(vmem, vmem),
-            scratch_shapes=[
-                pltpu.VMEM((envs, n, rows, rows), jnp.bfloat16),
-                pltpu.VMEM((envs, n, 2, rows // 2, rhs), jnp.bfloat16),
-                pltpu.VMEM((envs, rows, rhs), jnp.float32),
-                pltpu.VMEM((envs, rows, rhs), jnp.float32),
-                pltpu.VMEM((envs, 2, n, 4, rhs), jnp.float32),
-                pltpu.SemaphoreType.DMA((envs, n)),
-                pltpu.SemaphoreType.DMA((envs, 2, n, 2)),
-                pltpu.SemaphoreType.DMA((envs, n, 2)),
-                pltpu.SemaphoreType.DMA((envs, 2, n)),
-                pltpu.SemaphoreType.DMA((envs, 2, n)),
-            ],
-            compiler_params=pltpu.CompilerParams(
-                collective_id=0, has_side_effects=True, vmem_limit_bytes=60 * 1024 * 1024
-            ),
-        )(system_matrix, forces.transpose(1, 0, 2))
-        return x.transpose(1, 0, 2), r.transpose(1, 0, 2)
+        fits = envs == 2 and rhs == 128 and rows % (PIECES * rhs) == 0
+        if grid_of(n) == LADDER and mesh.shape["env"] % 2 == 0 and fits:
+            return ladder(n, LADDER[1], system_matrix, forces)
+        return ring(n, system_matrix, forces)
 
     return jax.shard_map(
         on_device,

time: 185 us -> 168 us (0.908)
  Pallas kernels: 176 us -> 163 us
  local copies, waits for them, and re-layouts: 8.27 us -> 4.52 us
    pallas_call x1, Pallas kernels: 176 us -> 163 us  [ladder(): pl.pallas_call(functools.partial(ladder_kernel, n, depth, rows), out_shap...]
    unnamed x3 -> x2, local copies, waits for them, and re-layouts: 8.27 us -> 4.52 us
where the time goes in v1:
time: 168 us
  Pallas kernels  163 us (97%)
  local copies, waits for them, and re-layouts  4.52 us (3%)
    pallas_call x1, Pallas kernels, ladder(): pl.pallas_call(functools.partial(ladder_kernel, n, depth, rows), out_shap...  163 us
    unnamed x2, local copies, waits for them, and re-layouts  4.52 us

profile of v1, /device:TPU:0, one launch (start us, length us, event | category | flops | bytes accessed | tf_op | source)
XLA Modules:
  0.0 168.1 jit_solution(14262612772248745188)
XLA Ops:
  0.6 163.0 %shard_map.41 = (f32[2048,128]{1,0:T(8,128)}, f32[2048,128]{1,0:T(8,128)}) custom-call(bf16[2,1024,8192]{2,1,0:T(8,128)(2,1)} %a_hbm.1, f32[2048,128]{1,0:T(8,128)} %bitcast.3), custom_call_target="tpu_custom_call" | custom-call | tf_op jit(solution)/shard_map/pallas_call | solution.py:688
  163.6 2.3 %copy.6 = f32[1024,2,128]{2,1,0:T(2,128)} copy(f32[1024,2,128]{2,1,0:T(2,128)} %bitcast.5) | data formatting | bytes 2097152
  165.9 2.3 %copy.7 = f32[1024,2,128]{2,1,0:T(2,128)} copy(f32[1024,2,128]{2,1,0:T(2,128)} %bitcast.4) | data formatting | bytes 2097152

commit v2 on v1

--- a/solution.py
+++ b/solution.py
@@ -34,16 +34,16 @@
 PIECES = 4
 LADDER = (2, 4)
 GATHER = (
-    (1, 2, 50, 145, 26, 137, 3, 36, 25, 43, 44, 52, 19, 60, 5, 38, 46, 27, 10, 13, 30, 22, 21, 23, 29, 31, 7, 15),
-    (160, 67, 100, 136, 75, 108, 116, 184, 219, 92, 102, 5, 144, 110, 145, 149, 126, 29, 1, 9, 86, 13, 87, 19, 95, 25, 7, 15),
+    (34, 137, 50, 145, 58, 36, 3, 12, 19, 43, 60, 27, 20, 38, 5, 54, 10, 62, 1, 29, 13, 7, 14, 21, 23, 31, 25, 15),
+    (160, 131, 68, 75, 108, 144, 116, 19, 184, 124, 70, 193, 136, 118, 137, 77, 126, 17, 85, 5, 78, 89, 79, 7, 27, 29, 23, 31),
 )
 SCATTER = (
-    (7, 15, 535, 543, 5, 10, 13, 21, 534, 29, 542, 515, 19, 539, 1, 514, 25, 538, 137, 550, 558, 548, 555, 556, 564, 145, 572, 562),
-    (7, 15, 531, 1, 5, 265, 13, 25, 541, 149, 599, 95, 598, 67, 401, 614, 638, 400, 622, 219, 612, 416, 440, 75, 620, 392, 628, 604),
+    (7, 527, 23, 31, 513, 5, 10, 525, 526, 533, 537, 29, 3, 524, 19, 532, 27, 145, 550, 566, 574, 546, 548, 555, 572, 137, 562, 570),
+    (519, 23, 31, 517, 273, 29, 19, 27, 193, 131, 591, 77, 590, 393, 85, 392, 89, 582, 630, 638, 620, 416, 628, 400, 580, 440, 75, 636),
 )
-OWN_SEND = ((5, 5, 5, 5), (7, 5, 6, 7))
-OWN_TAKE = ((5, 5, 5, 5), (7, 5, 6, 7))
-LEAVES = (18, 8)
+OWN_SEND = ((4, 5, 5, 4), (7, 5, 7, 7))
+OWN_TAKE = ((4, 5, 5, 4), (7, 5, 7, 7))
+LEAVES = (16, 8)
 GATHER_TURN = 20
 SCATTER_TURN = 28
 GROUP = 4
@@ -289,7 +289,7 @@
     update(1, ITERS - 1)
 
 
-def ladder_kernel(n, depth, rows, a_hbm, f_ref, x_out, r_out, a_gather, a_scatter,
+def ladder_kernel(n, depth, rows, a_hbm, f_ref, out, a_gather, a_scatter,
                   field, inbox, outbox, narrow, parts, xg, rg, dg, image, xs, rs, ds, drawn, sums,
                   load_sem, gather_send, gather_recv, scatter_send, scatter_recv, sum_send, sum_recv):
     width = 2
@@ -670,26 +670,26 @@
     @pl.when(core == 1)
     def _():
         gather_update(jnp.int32(ITERS))
-    x_out[strided(core, 0, rows), :] = xg[...]
-    r_out[strided(core, 0, rows), :] = rg[...]
+    out[0, strided(core, 0, rows), :] = xg[...]
+    out[1, strided(core, 0, rows), :] = rg[...]
     for q, lanes, at in cuts():
-        x_out[strided(other, at, rhs), :] = xs[q, :, lanes].T
-        r_out[strided(other, at, rhs), :] = rs[q, :, lanes].T
+        out[0, strided(other, at, rhs), :] = xs[q, :, lanes].T
+        out[1, strided(other, at, rhs), :] = rs[q, :, lanes].T
 
 
 def ladder(n, depth, system_matrix, forces):
     envs, rows, _ = system_matrix.shape
     rhs = forces.shape[-1]
     piece = rows // PIECES
-    flat = jax.ShapeDtypeStruct((rows * envs, rhs), jnp.float32)
+    both = jax.ShapeDtypeStruct((2, rows * envs, rhs), jnp.float32)
     vmem = pl.BlockSpec(memory_space=pltpu.VMEM)
     tall = pltpu.VMEM((rows, rhs), jnp.float32)
     wide = pltpu.VMEM((PIECES, rhs, piece), jnp.float32)
-    x, r = pl.pallas_call(
+    out = pl.pallas_call(
         functools.partial(ladder_kernel, n, depth, rows),
-        out_shape=(flat, flat),
+        out_shape=both,
         in_specs=[pl.BlockSpec(memory_space=pl.ANY), vmem],
-        out_specs=(vmem, vmem),
+        out_specs=vmem,
         scratch_shapes=[
             pltpu.VMEM((n, PIECES, rows, piece), jnp.bfloat16),
             pltpu.VMEM((n, PIECES, rows, piece), jnp.bfloat16),
@@ -713,7 +713,7 @@
             collective_id=0, has_side_effects=True, vmem_limit_bytes=62 * 1024 * 1024
         ),
     )(system_matrix, forces.reshape(rows * envs, rhs))
-    return x.reshape(rows, envs, rhs), r.reshape(rows, envs, rhs)
+    return out[0].reshape(rows, envs, rhs), out[1].reshape(rows, envs, rhs)
 
 
 def ring(n, system_matrix, forces):

time: 168 us -> 161 us (0.958)
  Pallas kernels: 163 us -> 158 us
    pallas_call x1, Pallas kernels: 163 us -> 158 us  [ladder(): pl.pallas_call(functools.partial(ladder_kernel, n, depth, rows), out_shap...]
    unnamed x2 -> x0, local copies, waits for them, and re-layouts: 4.52 us -> none
    slice x0 -> x1, local copies, waits for them, and re-layouts: none -> 2.99 us  [ladder(): return (out[0].reshape(rows, envs, rhs), out[1].reshape(rows, envs, rhs))]
where the time goes in v2:
time: 161 us
  Pallas kernels  158 us (98%)
  local copies, waits for them, and re-layouts  2.99 us (2%)
    pallas_call x1, Pallas kernels, ladder(): pl.pallas_call(functools.partial(ladder_kernel, n, depth, rows), out_shap...  158 us

profile of v2, /device:TPU:0, one launch (start us, length us, event | category | flops | bytes accessed | tf_op | source)
XLA Modules:
  0.0 161.3 jit_solution(2969562894222592004)
XLA Ops:
  0.6 157.7 %shard_map.41 = f32[2,2048,128]{2,1,0:T(8,128)} custom-call(bf16[2,1024,8192]{2,1,0:T(8,128)(2,1)} %a_hbm.1, f32[2048,128]{1,0:T(8,128)} %bitcast.3), custom_call_target="tpu_custom_call" | custom-call | tf_op jit(solution)/shard_map/pallas_call | solution.py:688
  158.3 3.0 %fusion = (f32[1,2048,128]{2,1,0:T(8,128)}, f32[1,2048,128]{2,1,0:T(8,128)}) fusion(f32[2,2048,128]{2,1,0:T(8,128)} %shard_map.41), kind=kLoop, calls=%fused_computation | loop fusion | bytes 4194304 | tf_op jit(solution)/shard_map/slice | solution.py:716
